TPU v7x, 128 devices: a whole 4x4x4 slice. The times are simulated.
128 devices in a mesh: utt: 8 (over y, core), clu: 16 (over z, x).
Axes of the slice: x: 4, y: 4, z: 4, core: 2. Of those that a mesh axis runs over, the one named last changes fastest.
Arguments:
- features: bfloat16 [262144, 1280], P(('utt', 'clu')), may hold values from -1.75 to 1.75
- centroids: bfloat16 [2048, 1280], P('clu'), may hold values from -2 to 2
- route: int32 [128, 128], P(('utt', 'clu')), may hold values from 0 to 127, each once within a row
Outputs:
- trainer_labels: int32 [128, 128, 16], P(('utt', 'clu'))
- trainer_distance: float32 [128, 128, 16], P(('utt', 'clu'))
Inputs may be any that keep to these rules, and one draw needn't show every extreme that they name: Each row of route names every trainer device exactly once.
All inputs are finite; a program needn't handle non-finite values.
Results may differ from a plain program's by a relative error of at most 0.0003.
Values may be sent and summed in bfloat16 or wider, within the bound.
No kernel may reach another device: no remote copies, remote signals or barrier semaphores. Data moves between devices by JAX's collectives and lax.ppermute only.
A program may use at most 64 MiB of HBM per device.

v0:
```python
import jax
import jax.numpy as jnp
from jax import lax
from jax.sharding import PartitionSpec as P


def per_device(features, centroids, route):
    rows = features.shape[0]
    width = features.shape[1]
    block = 512
    count = rows // block
    feat_blocks = features.reshape(count, block, width)
    frame_sq = jnp.sum(jnp.square(features.astype(jnp.float32)), axis=1).reshape(count, block)
    piece = lax.all_gather(centroids, "clu", axis=0, tiled=True)
    best_dist = jnp.full((count, block), jnp.inf, jnp.float32)
    best_index = jnp.zeros((count, block), jnp.int32)
    cent_sq = jnp.sum(jnp.square(piece.astype(jnp.float32)), axis=1)

    def one_block(items):
        feats, squares, held_dist, held_index = items
        inner = jnp.dot(feats, piece.T, preferred_element_type=jnp.float32)
        dist = (squares[:, None] - 2.0 * inner + cent_sq[None, :]) / width
        found = jnp.min(dist, axis=1)
        where = jnp.argmin(dist, axis=1)
        better = (found < held_dist) | (found == held_dist) & (where < held_index)
        return (jnp.where(better, found, held_dist), jnp.where(better, where, held_index))

    least, labels = lax.map(one_block, (feat_blocks, frame_sq, best_dist, best_index))
    n_utt = lax.axis_size("utt")
    n_clu = lax.axis_size("clu")
    devices = n_utt * n_clu
    per_block = rows // devices
    labels = labels.reshape(devices, per_block)
    least = least.reshape(devices, per_block)
    inverse = jnp.argsort(route[0])
    sent_labels = labels[inverse]
    sent_least = least[inverse]
    got_labels, got_least = (
        lax.all_to_all(sent_labels, ("utt", "clu"), split_axis=0, concat_axis=0, tiled=True),
        lax.all_to_all(sent_least, ("utt", "clu"), split_axis=0, concat_axis=0, tiled=True),
    )
    return (got_labels.reshape(1, devices, per_block), got_least.reshape(1, devices, per_block))


def solution(mesh):
    placed = (P(("utt", "clu"), None), P("clu", None), P(("utt", "clu"), None))
    return jax.shard_map(
        per_device,
        mesh=mesh,
        in_specs=placed,
        out_specs=(P(("utt", "clu"), None, None), P(("utt", "clu"), None, None)),
        check_vma=False,
    )
```

profile of v0, /device:TPU:1, one launch (start us, length us, event | category | flops | bytes accessed | tf_op | source)
XLA Modules:
  0.0 141.9 jit_solution(17112970766078503363)
XLA Ops:
  7.2 0.0 copy-start
  7.2 0.0 all-gather.2.cloned.1.call-start
  7.2 0.7 all-gather.2.cloned.1.call-update
  7.9 3.6 %multiply_reduce_fusion.1 = f32[2048]{0:T(1024)S(1)} fusion(bf16[2048,1280]{1,0:T(8,128)(2,1)} %param.5), kind=kLoop, calls=%fused_computation.11 | loop fusion | flops 7862272 | bytes 5251072 | tf_op jit(solution)/shard_map/reduce_sum | solution.py:13
  11.5 0.0 copy-done
  11.5 2.5 %sort.17 = (s32[128]{0:T(128)}, s32[128]{0:T(128)S(1)}) sort(s32[128]{0:T(128)S(1)} %bitcast.33, s32[128]{0:T(128)S(1)} %iota.11), dimensions={0}, to_apply=%region_5.6 | sort | flops 896 | bytes 2048 | tf_op jit(solution)/shard_map/jit(argsort)/sort | solution.py:35
  14.1 55.5 %all-gather.2.cloned.1.call-done = bf16[2048,1280]{1,0:T(8,128)(2,1)} async-done(((bf16[128,1280]{1,0:T(8,128)(2,1)}), bf16[2048,1280]{1,0:T(8,128)(2,1)}) %all-gather.2.cloned.1.call-update) | async-done | bytes 5242896 | tf_op jit(solution)/shard_map/all_gather | solution.py:14
  69.5 3.6 %multiply_reduce_fusion = f32[2048]{0:T(1024)S(1)} fusion(bf16[2048,1280]{1,0:T(8,128)(2,1)} %all-gather.2.cloned.1.call-done), kind=kLoop, calls=%fused_computation.10 | loop fusion | flops 7862272 | bytes 5251072 | tf_op jit(solution)/shard_map/reduce_sum | solution.py:17
  73.1 28.0 %while.12 = (s32[]{:T(128)}, f32[4,512]{1,0:T(4,128)S(1)}, s32[4,512]{1,0:T(4,128)S(1)}, f32[4,512]{1,0:T(4,128)S(1)}, bf16[4,512,1280]{2,1,0:T(8,128)(2,1)}, /*...) while((s32[]{:T(128)}, f32[4,512]{1,0:T(4,128)S(1)}, s32[4,512]{1,0:T(4,128)S(1)}, ...), condition=%wide.region_4.5_spmd, body=%wide.region_2.4_spmd.sunk | while | flops 2697987584 | bytes 6593129 | solution.py:28
  73.1 6.8 %iota_reduce_fusion.2 = (f32[512]{0:T(512)S(1)}, s32[512]{0:T(512)S(1)}) fusion(bf16[2048,1280]{1,0:T(8,128)(2,1)} %get-tuple-element.137, f32[2048]{0:T(1024)S(1)} %get-tuple-element.138, f32[512]{0:T(512)S(1)} %bitcast.32, bf16[4,512,1280]{2,1,0:T(8,128)(2,1)} %get-tuple-element.136, s32[]{:T(128)} %get-tuple-element.123), kind=kOutput, calls=%fused_computation.2.clone.1 | convolution fusion | flops 2697981440 | bytes 6568448 | tf_op jit(solution)/shard_map/while/body/eval_jaxpr/dot_general | solution.py:21
  80.0 0.1 dynamic_update_slice.11
  80.1 0.1 dynamic_update_slice.10
  80.1 6.8 %iota_reduce_fusion.2 = (f32[512]{0:T(512)S(1)}, s32[512]{0:T(512)S(1)}) fusion(bf16[2048,1280]{1,0:T(8,128)(2,1)} %get-tuple-element.137, f32[2048]{0:T(1024)S(1)} %get-tuple-element.138, f32[512]{0:T(512)S(1)} %bitcast.32, bf16[4,512,1280]{2,1,0:T(8,128)(2,1)} %get-tuple-element.136, s32[]{:T(128)} %get-tuple-element.123), kind=kOutput, calls=%fused_computation.2.clone.1 | convolution fusion | flops 2697981440 | bytes 6568448 | tf_op jit(solution)/shard_map/while/body/eval_jaxpr/dot_general | solution.py:21
  87.0 0.1 dynamic_update_slice.11
  87.0 0.1 dynamic_update_slice.10
  87.1 6.8 %iota_reduce_fusion.2 = (f32[512]{0:T(512)S(1)}, s32[512]{0:T(512)S(1)}) fusion(bf16[2048,1280]{1,0:T(8,128)(2,1)} %get-tuple-element.137, f32[2048]{0:T(1024)S(1)} %get-tuple-element.138, f32[512]{0:T(512)S(1)} %bitcast.32, bf16[4,512,1280]{2,1,0:T(8,128)(2,1)} %get-tuple-element.136, s32[]{:T(128)} %get-tuple-element.123), kind=kOutput, calls=%fused_computation.2.clone.1 | convolution fusion | flops 2697981440 | bytes 6568448 | tf_op jit(solution)/shard_map/while/body/eval_jaxpr/dot_general | solution.py:21
  94.0 0.1 dynamic_update_slice.11
  94.0 0.1 dynamic_update_slice.10
  94.1 6.8 %iota_reduce_fusion.2 = (f32[512]{0:T(512)S(1)}, s32[512]{0:T(512)S(1)}) fusion(bf16[2048,1280]{1,0:T(8,128)(2,1)} %get-tuple-element.137, f32[2048]{0:T(1024)S(1)} %get-tuple-element.138, f32[512]{0:T(512)S(1)} %bitcast.32, bf16[4,512,1280]{2,1,0:T(8,128)(2,1)} %get-tuple-element.136, s32[]{:T(128)} %get-tuple-element.123), kind=kOutput, calls=%fused_computation.2.clone.1 | convolution fusion | flops 2697981440 | bytes 6568448 | tf_op jit(solution)/shard_map/while/body/eval_jaxpr/dot_general | solution.py:21
  101.0 0.1 dynamic_update_slice.11
  101.0 0.1 dynamic_update_slice.10
  101.1 0.1 reshape.33
  101.2 1.2 gather_fusion
  102.4 8.0 %all-to-all-start = ((s32[128,1,16]{2,1,0:T(1,128)}), s32[128,1,16]{2,1,0:T(1,128)S(1)}, u32[]{:S(2)}, u32[]{:S(2)}) async-start(s32[128,1,16]{2,1,0:T(1,128)} %bitcast.7), calls=%async_computation | async-start | bytes 131072 | tf_op jit(solution)/shard_map/all_to_all | solution.py:39
  110.4 0.1 reshape.35
  110.5 1.2 gather_fusion.1
  111.8 8.5 %all-to-all-done = s32[128,1,16]{2,1,0:T(1,128)S(1)} async-done(((s32[128,1,16]{2,1,0:T(1,128)}), s32[128,1,16]{2,1,0:T(1,128)S(1)}, u32[]{:S(2)}, u32[]{:S(2)}) %all-to-all-start) | async-done | bytes 8224 | tf_op jit(solution)/shard_map/all_to_all | solution.py:39
  120.3 4.3 %all-to-all-start.1 = ((f32[128,1,16]{2,1,0:T(1,128)}), f32[128,1,16]{2,1,0:T(1,128)S(1)}, u32[]{:S(2)}, u32[]{:S(2)}) async-start(f32[128,1,16]{2,1,0:T(1,128)} %bitcast.10), calls=%async_computation.1 | async-start | bytes 131072 | tf_op jit(solution)/shard_map/all_to_all | solution.py:40
  124.5 0.7 copy.11
  125.2 9.1 %all-to-all-done.1 = f32[128,1,16]{2,1,0:T(1,128)S(1)} async-done(((f32[128,1,16]{2,1,0:T(1,128)}), f32[128,1,16]{2,1,0:T(1,128)S(1)}, u32[]{:S(2)}, u32[]{:S(2)}) %all-to-all-start.1) | async-done | bytes 8224 | tf_op jit(solution)/shard_map/all_to_all | solution.py:40
  134.4 0.7 copy.12
  (18 shorter events, 0.1 us)
Async XLA Ops:
  7.2 4.4 %copy-start = (s32[1,128]{1,0:T(1,128)S(1)}, s32[1,128]{1,0:T(1,128)}, u32[]{:S(2)}) copy-start(s32[1,128]{1,0:T(1,128)} %param.7) | copy-start | bytes 1540
  7.2 62.4 %all-gather.2.cloned.1.call-start = ((), (), s32[]{:S(2)}) async-start(), calls=%async_computation.2 | async-start | bytes 5570560 | tf_op jit(solution)/shard_map/all_gather | solution.py:14
  102.4 17.8 %all-to-all-start = ((s32[128,1,16]{2,1,0:T(1,128)}), s32[128,1,16]{2,1,0:T(1,128)S(1)}, u32[]{:S(2)}, u32[]{:S(2)}) async-start(s32[128,1,16]{2,1,0:T(1,128)} %bitcast.7), calls=%async_computation | async-start | bytes 131072 | tf_op jit(solution)/shard_map/all_to_all | solution.py:39
  120.3 14.1 %all-to-all-start.1 = ((f32[128,1,16]{2,1,0:T(1,128)}), f32[128,1,16]{2,1,0:T(1,128)S(1)}, u32[]{:S(2)}, u32[]{:S(2)}) async-start(f32[128,1,16]{2,1,0:T(1,128)} %bitcast.10), calls=%async_computation.1 | async-start | bytes 131072 | tf_op jit(solution)/shard_map/all_to_all | solution.py:40
Sparse Core Ops, SparseCore 0:
  10.1 59.3 all-gather.1
where the time goes:
time: 142 us
  waiting for transfers between devices  73.8 us (52%)
  matrix products  27.3 us (19%)
  between operations  14.1 us (10%)
  starting transfers between devices  12.3 us (9%)
  other arithmetic  9.75 us (7%)
  local copies, waits for them, and re-layouts  4.41 us (3%)
    all_gather x1, waiting for transfers between devices, per_device(): piece = lax.all_gather(centroids, 'clu', axis=0, tiled=True)  55.5 us
    dot_general x4, matrix products, one_block(): inner = jnp.dot(feats, piece.T, preferred_element_type=jnp.float32)  27.3 us
    all_to_all x1, waiting for transfers between devices, per_device(): lax.all_to_all(sent_least, ('utt', 'clu'), split_axis=0, concat_axis=0, t...  9.14 us
    all_to_all x1, waiting for transfers between devices, per_device(): lax.all_to_all(sent_labels, ('utt', 'clu'), split_axis=0, concat_axis=0,...  8.49 us
    all_to_all x1, starting transfers between devices, per_device(): lax.all_to_all(sent_labels, ('utt', 'clu'), split_axis=0, concat_axis=0,...  8.03 us
    all_to_all x1, starting transfers between devices, per_device(): lax.all_to_all(sent_least, ('utt', 'clu'), split_axis=0, concat_axis=0, t...  4.28 us
    reduce_sum x1, other arithmetic, per_device(): jnp.sum(jnp.square(features.astype(jnp.float32)), axis=1)  3.58 us
    reduce_sum x1, other arithmetic, per_device(): cent_sq = jnp.sum(jnp.square(piece.astype(jnp.float32)), axis=1)  3.58 us
  transfers between devices with their start and end apart: 3, of which 3 were waited for; matrix products, arithmetic and copies ran while one was open for 6% of the time, Pallas kernels for 0%

commit v1 on v0

--- a/solution.py
+++ b/solution.py
@@ -1,7 +1,39 @@
+import functools
 import jax
 import jax.numpy as jnp
 from jax import lax
 from jax.sharding import PartitionSpec as P
+from jax.lax import axis_index, axis_size, ppermute
+
+
+def time_the_gates(local_x, pos_dim):
+    w2, earlier, mid_arr = (axis_size("clu"), axis_index("clu"), local_x.shape[pos_dim])
+    kept_rows = list(map(lambda dd: (dd, (dd + 1) % w2), range(w2)))
+    later = range(w2)
+    vec_out = map(lambda dd: (dd, (dd - 1) % w2), later)
+    pool = list(vec_out)
+    val2 = jnp.zeros(
+        (*local_x.shape[:pos_dim], w2 * mid_arr, *local_x.shape[pos_dim + 1 :]), local_x.dtype
+    )
+    val2 = lax.dynamic_update_slice_in_dim(val2, local_x, earlier * mid_arr, axis=pos_dim)
+    step_out = res = local_x
+    mixed_arr = w2 // 2
+    h = 1
+    while h < mixed_arr + 1:
+        step_out = ppermute(step_out, "clu", kept_rows)
+        val2 = lax.dynamic_update_slice_in_dim(
+            val2, step_out, (earlier - h) % w2 * mid_arr, axis=pos_dim
+        )
+        if h < w2 - mixed_arr:
+            res = ppermute(res, "clu", pool)
+            val2 = lax.dynamic_update_slice_in_dim(
+                val2, res, (earlier + h) % w2 * mid_arr, axis=pos_dim
+            )
+        h = h + 1
+    return val2
+
+
+unit_prepare = functools.partial(time_the_gates, pos_dim=0)
 
 
 def per_device(features, centroids, route):
@@ -11,7 +43,7 @@
     count = rows // block
     feat_blocks = features.reshape(count, block, width)
     frame_sq = jnp.sum(jnp.square(features.astype(jnp.float32)), axis=1).reshape(count, block)
-    piece = lax.all_gather(centroids, "clu", axis=0, tiled=True)
+    piece = unit_prepare(centroids)
     best_dist = jnp.full((count, block), jnp.inf, jnp.float32)
     best_index = jnp.zeros((count, block), jnp.int32)
     cent_sq = jnp.sum(jnp.square(piece.astype(jnp.float32)), axis=1)

time: 142 us -> 153 us (1.077)
  starting transfers between devices: 12.3 us -> 52.4 us
  waiting for transfers between devices: 73.8 us -> 58.6 us
  between operations: 14.1 us -> 0.83 us
  other arithmetic: 9.75 us -> 7.31 us
  local copies, waits for them, and re-layouts: 4.41 us -> 6.41 us
    all_gather x1 -> x0, waiting for transfers between devices: 55.5 us -> none  [per_device(): piece = lax.all_gather(centroids, 'clu', axis=0, tiled=True)]
    ppermute x0 -> x15, waiting for transfers between devices: none -> 41 us  [the longest x8 41 us: time_the_gates(): step_out = ppermute(step_out, 'clu', kept_rows)]
    ppermute x0 -> x15, starting transfers between devices: none -> 35.6 us  [the longest x7 33.5 us: time_the_gates(): res = ppermute(res, 'clu', pool)]
    all_to_all x1, starting transfers between devices: 8.03 us -> 12.5 us  [per_device(): lax.all_to_all(sent_labels, ('utt', 'clu'), split_axis=0, concat_axis=0,...]
    reduce_sum x1, other arithmetic: 3.58 us -> 1.09 us  [per_device(): cent_sq = jnp.sum(jnp.square(piece.astype(jnp.float32)), axis=1)]
  transfers between devices with their start and end apart: 3 -> 17, of which waited for: 3 -> 10; matrix products, arithmetic and copies ran while one was open for 6% -> 6% of each run, Pallas kernels for 0% -> 0%
where the time goes in v1:
time: 153 us
  waiting for transfers between devices  58.6 us (38%)
  starting transfers between devices  52.4 us (34%)
  matrix products  27.3 us (18%)
  other arithmetic  7.31 us (5%)
  local copies, waits for them, and re-layouts  6.41 us (4%)
    ppermute x8, waiting for transfers between devices, time_the_gates(): step_out = ppermute(step_out, 'clu', kept_rows)  41 us
    ppermute x7, starting transfers between devices, time_the_gates(): res = ppermute(res, 'clu', pool)  33.5 us
    dot_general x4, matrix products, one_block(): inner = jnp.dot(feats, piece.T, preferred_element_type=jnp.float32)  27.3 us
    all_to_all x1, starting transfers between devices, per_device(): lax.all_to_all(sent_labels, ('utt', 'clu'), split_axis=0, concat_axis=0,...  12.5 us
    all_to_all x1, waiting for transfers between devices, per_device(): lax.all_to_all(sent_least, ('utt', 'clu'), split_axis=0, concat_axis=0, t...  9.14 us
    all_to_all x1, waiting for transfers between devices, per_device(): lax.all_to_all(sent_labels, ('utt', 'clu'), split_axis=0, concat_axis=0,...  8.49 us
    all_to_all x1, starting transfers between devices, per_device(): lax.all_to_all(sent_least, ('utt', 'clu'), split_axis=0, concat_axis=0, t...  4.28 us
    reduce_sum x1, other arithmetic, per_device(): jnp.sum(jnp.square(features.astype(jnp.float32)), axis=1)  3.62 us
  transfers between devices with their start and end apart: 17, of which 10 were waited for; matrix products, arithmetic and copies ran while one was open for 6% of the time, Pallas kernels for 0%

profile of v1, /device:TPU:1, one launch (start us, length us, event | category | flops | bytes accessed | tf_op | source)
XLA Modules:
  0.0 153.1 jit_solution(16636548554991904617)
XLA Ops:
  0.6 2.1 %collective-permute-start = (bf16[128,1280]{1,0:T(8,128)(2,1)}, bf16[128,1280]{1,0:T(8,128)(2,1)S(1)}, u32[]{:S(2)}, u32[]{:S(2)}) collective-permute-start(bf16[128,1280]{1,0:T(8,128)(2,1)} %param.6), channel_id=1, source_target_pairs={{0,1},{1,2},{2,3},{3,4},{4,5},{5,6},{6,7},{7,8},{8,9},{9,10},{10,1... | collective-permute-start | bytes 983048 | tf_op jit(solution)/shard_map/ppermute | solution.py:23
  2.7 4.8 %collective-permute-start.1 = (bf16[128,1280]{1,0:T(8,128)(2,1)}, bf16[128,1280]{1,0:T(8,128)(2,1)S(1)}, u32[]{:S(2)}, u32[]{:S(2)}) collective-permute-start(bf16[128,1280]{1,0:T(8,128)(2,1)} %param.6), channel_id=1, source_target_pairs={{0,15},{1,0},{2,1},{3,2},{4,3},{5,4},{6,5},{7,6},{8,7},{9,8},{10,9... | collective-permute-start | bytes 983048 | tf_op jit(solution)/shard_map/ppermute | solution.py:28
  7.6 3.6 %multiply_reduce_fusion.1 = f32[2048]{0:T(1024)S(1)} fusion(bf16[2048,1280]{1,0:T(8,128)(2,1)} %param.5), kind=kLoop, calls=%fused_computation.11 | loop fusion | flops 7862272 | bytes 5251072 | tf_op jit(solution)/shard_map/reduce_sum | solution.py:45
  11.2 2.5 %sort.17 = (s32[128]{0:T(128)}, s32[128]{0:T(128)S(1)}) sort(s32[128]{0:T(128)S(1)} %bitcast.33, s32[128]{0:T(128)S(1)} %iota.11), dimensions={0}, to_apply=%region_5.6 | sort | flops 896 | bytes 2048 | tf_op jit(solution)/shard_map/jit(argsort)/sort | solution.py:67
  14.2 0.9 collective-permute-done
  15.1 4.8 %collective-permute-start.3 = (bf16[128,1280]{1,0:T(8,128)(2,1)S(1)}, bf16[128,1280]{1,0:T(8,128)(2,1)S(1)}, u32[]{:S(2)}, u32[]{:S(2)}) collective-permute-start(bf16[128,1280]{1,0:T(8,128)(2,1)S(1)} %collective-permute-done.1), channel_id=1, source_target_pairs={{0,15},{1,0},{2,1},{3,2},{4,3},{5,4},{6,5},{7,6},{8,7},{9,8},{10,9... | collective-permute-start | bytes 983048 | tf_op jit(solution)/shard_map/ppermute | solution.py:28
  20.0 6.5 %collective-permute-done.2 = bf16[128,1280]{1,0:T(8,128)(2,1)S(1)} collective-permute-done((bf16[128,1280]{1,0:T(8,128)(2,1)S(1)}, bf16[128,1280]{1,0:T(8,128)(2,1)S(1)}, u32[]{:S(2)}, u32[]{:S(2)}) %collective-permute-start.2) | collective-permute-done | bytes 327712 | tf_op jit(solution)/shard_map/ppermute | solution.py:23
  26.5 4.8 %collective-permute-start.5 = (bf16[128,1280]{1,0:T(8,128)(2,1)S(1)}, bf16[128,1280]{1,0:T(8,128)(2,1)S(1)}, u32[]{:S(2)}, u32[]{:S(2)}) collective-permute-start(bf16[128,1280]{1,0:T(8,128)(2,1)S(1)} %collective-permute-done.3), channel_id=1, source_target_pairs={{0,15},{1,0},{2,1},{3,2},{4,3},{5,4},{6,5},{7,6},{8,7},{9,8},{10,9... | collective-permute-start | bytes 983048 | tf_op jit(solution)/shard_map/ppermute | solution.py:28
  31.3 5.6 %collective-permute-done.4 = bf16[128,1280]{1,0:T(8,128)(2,1)S(1)} collective-permute-done((bf16[128,1280]{1,0:T(8,128)(2,1)S(1)}, bf16[128,1280]{1,0:T(8,128)(2,1)S(1)}, u32[]{:S(2)}, u32[]{:S(2)}) %collective-permute-start.4) | collective-permute-done | bytes 327712 | tf_op jit(solution)/shard_map/ppermute | solution.py:23
  36.9 4.8 %collective-permute-start.7 = (bf16[128,1280]{1,0:T(8,128)(2,1)S(1)}, bf16[128,1280]{1,0:T(8,128)(2,1)S(1)}, u32[]{:S(2)}, u32[]{:S(2)}) collective-permute-start(bf16[128,1280]{1,0:T(8,128)(2,1)S(1)} %collective-permute-done.5), channel_id=1, source_target_pairs={{0,15},{1,0},{2,1},{3,2},{4,3},{5,4},{6,5},{7,6},{8,7},{9,8},{10,9... | collective-permute-start | bytes 983048 | tf_op jit(solution)/shard_map/ppermute | solution.py:28
  41.8 4.8 %collective-permute-done.6 = bf16[128,1280]{1,0:T(8,128)(2,1)S(1)} collective-permute-done((bf16[128,1280]{1,0:T(8,128)(2,1)S(1)}, bf16[128,1280]{1,0:T(8,128)(2,1)S(1)}, u32[]{:S(2)}, u32[]{:S(2)}) %collective-permute-start.6) | collective-permute-done | bytes 327712 | tf_op jit(solution)/shard_map/ppermute | solution.py:23
  46.6 4.8 %collective-permute-start.9 = (bf16[128,1280]{1,0:T(8,128)(2,1)S(1)}, bf16[128,1280]{1,0:T(8,128)(2,1)S(1)}, u32[]{:S(2)}, u32[]{:S(2)}) collective-permute-start(bf16[128,1280]{1,0:T(8,128)(2,1)S(1)} %collective-permute-done.7), channel_id=1, source_target_pairs={{0,15},{1,0},{2,1},{3,2},{4,3},{5,4},{6,5},{7,6},{8,7},{9,8},{10,9... | collective-permute-start | bytes 983048 | tf_op jit(solution)/shard_map/ppermute | solution.py:28
  51.4 4.4 %collective-permute-done.8 = bf16[128,1280]{1,0:T(8,128)(2,1)S(1)} collective-permute-done((bf16[128,1280]{1,0:T(8,128)(2,1)S(1)}, bf16[128,1280]{1,0:T(8,128)(2,1)S(1)}, u32[]{:S(2)}, u32[]{:S(2)}) %collective-permute-start.8) | collective-permute-done | bytes 327712 | tf_op jit(solution)/shard_map/ppermute | solution.py:23
  55.8 4.8 %collective-permute-start.11 = (bf16[128,1280]{1,0:T(8,128)(2,1)S(1)}, bf16[128,1280]{1,0:T(8,128)(2,1)S(1)}, u32[]{:S(2)}, u32[]{:S(2)}) collective-permute-start(bf16[128,1280]{1,0:T(8,128)(2,1)S(1)} %collective-permute-done.9), channel_id=1, source_target_pairs={{0,15},{1,0},{2,1},{3,2},{4,3},{5,4},{6,5},{7,6},{8,7},{9,8},{10,9... | collective-permute-start | bytes 983048 | tf_op jit(solution)/shard_map/ppermute | solution.py:28
  60.7 4.4 %collective-permute-done.10 = bf16[128,1280]{1,0:T(8,128)(2,1)S(1)} collective-permute-done((bf16[128,1280]{1,0:T(8,128)(2,1)S(1)}, bf16[128,1280]{1,0:T(8,128)(2,1)S(1)}, u32[]{:S(2)}, u32[]{:S(2)}) %collective-permute-start.10) | collective-permute-done | bytes 327712 | tf_op jit(solution)/shard_map/ppermute | solution.py:23
  65.1 4.8 %collective-permute-start.13 = (bf16[128,1280]{1,0:T(8,128)(2,1)S(1)}, bf16[128,1280]{1,0:T(8,128)(2,1)S(1)}, u32[]{:S(2)}, u32[]{:S(2)}) collective-permute-start(bf16[128,1280]{1,0:T(8,128)(2,1)S(1)} %collective-permute-done.11), channel_id=1, source_target_pairs={{0,15},{1,0},{2,1},{3,2},{4,3},{5,4},{6,5},{7,6},{8,7},{9,8},{10,9... | collective-permute-start | bytes 983048 | tf_op jit(solution)/shard_map/ppermute | solution.py:28
  69.9 4.4 %collective-permute-done.12 = bf16[128,1280]{1,0:T(8,128)(2,1)S(1)} collective-permute-done((bf16[128,1280]{1,0:T(8,128)(2,1)S(1)}, bf16[128,1280]{1,0:T(8,128)(2,1)S(1)}, u32[]{:S(2)}, u32[]{:S(2)}) %collective-permute-start.12) | collective-permute-done | bytes 327712 | tf_op jit(solution)/shard_map/ppermute | solution.py:23
  74.4 10.0 %collective-permute-done.14 = bf16[128,1280]{1,0:T(8,128)(2,1)S(1)} collective-permute-done((bf16[128,1280]{1,0:T(8,128)(2,1)S(1)}, bf16[128,1280]{1,0:T(8,128)(2,1)S(1)}, u32[]{:S(2)}, u32[]{:S(2)}) %collective-permute-start.14) | collective-permute-done | bytes 327712 | tf_op jit(solution)/shard_map/ppermute | solution.py:23
  84.4 1.1 multiply_reduce_fusion
  85.5 1.2 copy-done
  86.7 28.0 %while.12 = (s32[]{:T(128)}, f32[4,512]{1,0:T(4,128)S(1)}, s32[4,512]{1,0:T(4,128)S(1)}, f32[4,512]{1,0:T(4,128)S(1)}, bf16[4,512,1280]{2,1,0:T(8,128)(2,1)}, /*...) while((s32[]{:T(128)}, f32[4,512]{1,0:T(4,128)S(1)}, s32[4,512]{1,0:T(4,128)S(1)}, ...), condition=%wide.region_4.5_spmd, body=%wide.region_2.4_spmd.sunk | while | flops 2697987584 | bytes 6593129 | solution.py:60
  86.7 6.8 %iota_reduce_fusion.2 = (f32[512]{0:T(512)S(1)}, s32[512]{0:T(512)S(1)}) fusion(bf16[2048,1280]{1,0:T(8,128)(2,1)} %get-tuple-element.137, f32[2048]{0:T(1024)S(1)} %get-tuple-element.138, f32[512]{0:T(512)S(1)} %bitcast.32, bf16[4,512,1280]{2,1,0:T(8,128)(2,1)} %get-tuple-element.136, s32[]{:T(128)} %get-tuple-element.123), kind=kOutput, calls=%fused_computation.2.clone.1 | convolution fusion | flops 2697981440 | bytes 6568448 | tf_op jit(solution)/shard_map/while/body/eval_jaxpr/dot_general | solution.py:53
  93.7 6.8 %iota_reduce_fusion.2 = (f32[512]{0:T(512)S(1)}, s32[512]{0:T(512)S(1)}) fusion(bf16[2048,1280]{1,0:T(8,128)(2,1)} %get-tuple-element.137, f32[2048]{0:T(1024)S(1)} %get-tuple-element.138, f32[512]{0:T(512)S(1)} %bitcast.32, bf16[4,512,1280]{2,1,0:T(8,128)(2,1)} %get-tuple-element.136, s32[]{:T(128)} %get-tuple-element.123), kind=kOutput, calls=%fused_computation.2.clone.1 | convolution fusion | flops 2697981440 | bytes 6568448 | tf_op jit(solution)/shard_map/while/body/eval_jaxpr/dot_general | solution.py:53
  100.7 6.8 %iota_reduce_fusion.2 = (f32[512]{0:T(512)S(1)}, s32[512]{0:T(512)S(1)}) fusion(bf16[2048,1280]{1,0:T(8,128)(2,1)} %get-tuple-element.137, f32[2048]{0:T(1024)S(1)} %get-tuple-element.138, f32[512]{0:T(512)S(1)} %bitcast.32, bf16[4,512,1280]{2,1,0:T(8,128)(2,1)} %get-tuple-element.136, s32[]{:T(128)} %get-tuple-element.123), kind=kOutput, calls=%fused_computation.2.clone.1 | convolution fusion | flops 2697981440 | bytes 6568448 | tf_op jit(solution)/shard_map/while/body/eval_jaxpr/dot_general | solution.py:53
  107.7 6.8 %iota_reduce_fusion.2 = (f32[512]{0:T(512)S(1)}, s32[512]{0:T(512)S(1)}) fusion(bf16[2048,1280]{1,0:T(8,128)(2,1)} %get-tuple-element.137, f32[2048]{0:T(1024)S(1)} %get-tuple-element.138, f32[512]{0:T(512)S(1)} %bitcast.32, bf16[4,512,1280]{2,1,0:T(8,128)(2,1)} %get-tuple-element.136, s32[]{:T(128)} %get-tuple-element.123), kind=kOutput, calls=%fused_computation.2.clone.1 | convolution fusion | flops 2697981440 | bytes 6568448 | tf_op jit(solution)/shard_map/while/body/eval_jaxpr/dot_general | solution.py:53
  114.8 1.2 gather_fusion
  116.0 12.5 %all-to-all-start = ((s32[128,1,16]{2,1,0:T(1,128)}), s32[128,1,16]{2,1,0:T(1,128)S(1)}, u32[]{:S(2)}, u32[]{:S(2)}) async-start(s32[128,1,16]{2,1,0:T(1,128)} %bitcast.7), calls=%async_computation | async-start | bytes 131072 | tf_op jit(solution)/shard_map/all_to_all | solution.py:71
  128.6 1.2 gather_fusion.1
  129.8 8.5 %all-to-all-done = s32[128,1,16]{2,1,0:T(1,128)S(1)} async-done(((s32[128,1,16]{2,1,0:T(1,128)}), s32[128,1,16]{2,1,0:T(1,128)S(1)}, u32[]{:S(2)}, u32[]{:S(2)}) %all-to-all-start) | async-done | bytes 8224 | tf_op jit(solution)/shard_map/all_to_all | solution.py:71
  138.3 4.3 %all-to-all-start.1 = ((f32[128,1,16]{2,1,0:T(1,128)}), f32[128,1,16]{2,1,0:T(1,128)S(1)}, u32[]{:S(2)}, u32[]{:S(2)}) async-start(f32[128,1,16]{2,1,0:T(1,128)} %bitcast.10), calls=%async_computation.1 | async-start | bytes 131072 | tf_op jit(solution)/shard_map/all_to_all | solution.py:72
  142.6 0.7 copy.11
  143.3 9.1 %all-to-all-done.1 = f32[128,1,16]{2,1,0:T(1,128)S(1)} async-done(((f32[128,1,16]{2,1,0:T(1,128)}), f32[128,1,16]{2,1,0:T(1,128)S(1)}, u32[]{:S(2)}, u32[]{:S(2)}) %all-to-all-start.1) | async-done | bytes 8224 | tf_op jit(solution)/shard_map/all_to_all | solution.py:72
  (65 shorter events, 2.2 us)
Async XLA Ops:
  0.6 10.6 %copy-start.2 = (s32[1,128]{1,0:T(1,128)S(1)}, s32[1,128]{1,0:T(1,128)}, u32[]{:S(2)}) copy-start(s32[1,128]{1,0:T(1,128)} %param.7) | copy-start | bytes 1540
  0.6 14.5 %collective-permute-start = (bf16[128,1280]{1,0:T(8,128)(2,1)}, bf16[128,1280]{1,0:T(8,128)(2,1)S(1)}, u32[]{:S(2)}, u32[]{:S(2)}) collective-permute-start(bf16[128,1280]{1,0:T(8,128)(2,1)} %param.6), channel_id=1, source_target_pairs={{0,1},{1,2},{2,3},{3,4},{4,5},{5,6},{6,7},{7,8},{8,9},{9,10},{10,1... | collective-permute-start | bytes 983048 | tf_op jit(solution)/shard_map/ppermute | solution.py:23
  2.7 12.4 %collective-permute-start.1 = (bf16[128,1280]{1,0:T(8,128)(2,1)}, bf16[128,1280]{1,0:T(8,128)(2,1)S(1)}, u32[]{:S(2)}, u32[]{:S(2)}) collective-permute-start(bf16[128,1280]{1,0:T(8,128)(2,1)} %param.6), channel_id=1, source_target_pairs={{0,15},{1,0},{2,1},{3,2},{4,3},{5,4},{6,5},{7,6},{8,7},{9,8},{10,9... | collective-permute-start | bytes 983048 | tf_op jit(solution)/shard_map/ppermute | solution.py:28
  7.6 6.6 %copy-start.1 = (bf16[128,1280]{1,0:T(8,128)(2,1)S(1)}, bf16[128,1280]{1,0:T(8,128)(2,1)}, u32[]{:S(2)}) copy-start(bf16[128,1280]{1,0:T(8,128)(2,1)} %param.6) | copy-start | bytes 983044
  15.1 11.3 %collective-permute-start.2 = (bf16[128,1280]{1,0:T(8,128)(2,1)S(1)}, bf16[128,1280]{1,0:T(8,128)(2,1)S(1)}, u32[]{:S(2)}, u32[]{:S(2)}) collective-permute-start(bf16[128,1280]{1,0:T(8,128)(2,1)S(1)} %collective-permute-done), channel_id=1, source_target_pairs={{0,1},{1,2},{2,3},{3,4},{4,5},{5,6},{6,7},{7,8},{8,9},{9,10},{10,1... | collective-permute-start | bytes 983048 | tf_op jit(solution)/shard_map/ppermute | solution.py:23
  15.1 11.3 %collective-permute-start.3 = (bf16[128,1280]{1,0:T(8,128)(2,1)S(1)}, bf16[128,1280]{1,0:T(8,128)(2,1)S(1)}, u32[]{:S(2)}, u32[]{:S(2)}) collective-permute-start(bf16[128,1280]{1,0:T(8,128)(2,1)S(1)} %collective-permute-done.1), channel_id=1, source_target_pairs={{0,15},{1,0},{2,1},{3,2},{4,3},{5,4},{6,5},{7,6},{8,7},{9,8},{10,9... | collective-permute-start | bytes 983048 | tf_op jit(solution)/shard_map/ppermute | solution.py:28
  26.4 10.5 %collective-permute-start.4 = (bf16[128,1280]{1,0:T(8,128)(2,1)S(1)}, bf16[128,1280]{1,0:T(8,128)(2,1)S(1)}, u32[]{:S(2)}, u32[]{:S(2)}) collective-permute-start(bf16[128,1280]{1,0:T(8,128)(2,1)S(1)} %collective-permute-done.2), channel_id=1, source_target_pairs={{0,1},{1,2},{2,3},{3,4},{4,5},{5,6},{6,7},{7,8},{8,9},{9,10},{10,1... | collective-permute-start | bytes 983048 | tf_op jit(solution)/shard_map/ppermute | solution.py:23
  26.5 10.5 %collective-permute-start.5 = (bf16[128,1280]{1,0:T(8,128)(2,1)S(1)}, bf16[128,1280]{1,0:T(8,128)(2,1)S(1)}, u32[]{:S(2)}, u32[]{:S(2)}) collective-permute-start(bf16[128,1280]{1,0:T(8,128)(2,1)S(1)} %collective-permute-done.3), channel_id=1, source_target_pairs={{0,15},{1,0},{2,1},{3,2},{4,3},{5,4},{6,5},{7,6},{8,7},{9,8},{10,9... | collective-permute-start | bytes 983048 | tf_op jit(solution)/shard_map/ppermute | solution.py:28
  36.9 9.6 %collective-permute-start.6 = (bf16[128,1280]{1,0:T(8,128)(2,1)S(1)}, bf16[128,1280]{1,0:T(8,128)(2,1)S(1)}, u32[]{:S(2)}, u32[]{:S(2)}) collective-permute-start(bf16[128,1280]{1,0:T(8,128)(2,1)S(1)} %collective-permute-done.4), channel_id=1, source_target_pairs={{0,1},{1,2},{2,3},{3,4},{4,5},{5,6},{6,7},{7,8},{8,9},{9,10},{10,1... | collective-permute-start | bytes 983048 | tf_op jit(solution)/shard_map/ppermute | solution.py:23
  36.9 9.6 %collective-permute-start.7 = (bf16[128,1280]{1,0:T(8,128)(2,1)S(1)}, bf16[128,1280]{1,0:T(8,128)(2,1)S(1)}, u32[]{:S(2)}, u32[]{:S(2)}) collective-permute-start(bf16[128,1280]{1,0:T(8,128)(2,1)S(1)} %collective-permute-done.5), channel_id=1, source_target_pairs={{0,15},{1,0},{2,1},{3,2},{4,3},{5,4},{6,5},{7,6},{8,7},{9,8},{10,9... | collective-permute-start | bytes 983048 | tf_op jit(solution)/shard_map/ppermute | solution.py:28
  46.6 9.2 %collective-permute-start.8 = (bf16[128,1280]{1,0:T(8,128)(2,1)S(1)}, bf16[128,1280]{1,0:T(8,128)(2,1)S(1)}, u32[]{:S(2)}, u32[]{:S(2)}) collective-permute-start(bf16[128,1280]{1,0:T(8,128)(2,1)S(1)} %collective-permute-done.6), channel_id=1, source_target_pairs={{0,1},{1,2},{2,3},{3,4},{4,5},{5,6},{6,7},{7,8},{8,9},{9,10},{10,1... | collective-permute-start | bytes 983048 | tf_op jit(solution)/shard_map/ppermute | solution.py:23
  46.6 9.2 %collective-permute-start.9 = (bf16[128,1280]{1,0:T(8,128)(2,1)S(1)}, bf16[128,1280]{1,0:T(8,128)(2,1)S(1)}, u32[]{:S(2)}, u32[]{:S(2)}) collective-permute-start(bf16[128,1280]{1,0:T(8,128)(2,1)S(1)} %collective-permute-done.7), channel_id=1, source_target_pairs={{0,15},{1,0},{2,1},{3,2},{4,3},{5,4},{6,5},{7,6},{8,7},{9,8},{10,9... | collective-permute-start | bytes 983048 | tf_op jit(solution)/shard_map/ppermute | solution.py:28
  55.8 9.2 %collective-permute-start.10 = (bf16[128,1280]{1,0:T(8,128)(2,1)S(1)}, bf16[128,1280]{1,0:T(8,128)(2,1)S(1)}, u32[]{:S(2)}, u32[]{:S(2)}) collective-permute-start(bf16[128,1280]{1,0:T(8,128)(2,1)S(1)} %collective-permute-done.8), channel_id=1, source_target_pairs={{0,1},{1,2},{2,3},{3,4},{4,5},{5,6},{6,7},{7,8},{8,9},{9,10},{10,1... | collective-permute-start | bytes 983048 | tf_op jit(solution)/shard_map/ppermute | solution.py:23
  55.8 9.2 %collective-permute-start.11 = (bf16[128,1280]{1,0:T(8,128)(2,1)S(1)}, bf16[128,1280]{1,0:T(8,128)(2,1)S(1)}, u32[]{:S(2)}, u32[]{:S(2)}) collective-permute-start(bf16[128,1280]{1,0:T(8,128)(2,1)S(1)} %collective-permute-done.9), channel_id=1, source_target_pairs={{0,15},{1,0},{2,1},{3,2},{4,3},{5,4},{6,5},{7,6},{8,7},{9,8},{10,9... | collective-permute-start | bytes 983048 | tf_op jit(solution)/shard_map/ppermute | solution.py:28
  65.0 9.2 %collective-permute-start.12 = (bf16[128,1280]{1,0:T(8,128)(2,1)S(1)}, bf16[128,1280]{1,0:T(8,128)(2,1)S(1)}, u32[]{:S(2)}, u32[]{:S(2)}) collective-permute-start(bf16[128,1280]{1,0:T(8,128)(2,1)S(1)} %collective-permute-done.10), channel_id=1, source_target_pairs={{0,1},{1,2},{2,3},{3,4},{4,5},{5,6},{6,7},{7,8},{8,9},{9,10},{10,1... | collective-permute-start | bytes 983048 | tf_op jit(solution)/shard_map/ppermute | solution.py:23
  65.1 9.3 %collective-permute-start.13 = (bf16[128,1280]{1,0:T(8,128)(2,1)S(1)}, bf16[128,1280]{1,0:T(8,128)(2,1)S(1)}, u32[]{:S(2)}, u32[]{:S(2)}) collective-permute-start(bf16[128,1280]{1,0:T(8,128)(2,1)S(1)} %collective-permute-done.11), channel_id=1, source_target_pairs={{0,15},{1,0},{2,1},{3,2},{4,3},{5,4},{6,5},{7,6},{8,7},{9,8},{10,9... | collective-permute-start | bytes 983048 | tf_op jit(solution)/shard_map/ppermute | solution.py:28
  74.3 10.1 %collective-permute-start.14 = (bf16[128,1280]{1,0:T(8,128)(2,1)S(1)}, bf16[128,1280]{1,0:T(8,128)(2,1)S(1)}, u32[]{:S(2)}, u32[]{:S(2)}) collective-permute-start(bf16[128,1280]{1,0:T(8,128)(2,1)S(1)} %collective-permute-done.12), channel_id=1, source_target_pairs={{0,1},{1,2},{2,3},{3,4},{4,5},{5,6},{6,7},{7,8},{8,9},{9,10},{10,1... | collective-permute-start | bytes 983048 | tf_op jit(solution)/shard_map/ppermute | solution.py:23
  84.4 2.3 %copy-start = (bf16[2048,1280]{1,0:T(8,128)(2,1)}, bf16[2048,1280]{1,0:T(8,128)(2,1)S(1)}, u32[]{:S(2)}) copy-start(bf16[2048,1280]{1,0:T(8,128)(2,1)S(1)} %constant_dynamic-update-slice_fusion) | copy-start | bytes 15728644
  116.0 22.3 %all-to-all-start = ((s32[128,1,16]{2,1,0:T(1,128)}), s32[128,1,16]{2,1,0:T(1,128)S(1)}, u32[]{:S(2)}, u32[]{:S(2)}) async-start(s32[128,1,16]{2,1,0:T(1,128)} %bitcast.7), calls=%async_computation | async-start | bytes 131072 | tf_op jit(solution)/shard_map/all_to_all | solution.py:71
  138.3 14.1 %all-to-all-start.1 = ((f32[128,1,16]{2,1,0:T(1,128)}), f32[128,1,16]{2,1,0:T(1,128)S(1)}, u32[]{:S(2)}, u32[]{:S(2)}) async-start(f32[128,1,16]{2,1,0:T(1,128)} %bitcast.10), calls=%async_computation.1 | async-start | bytes 131072 | tf_op jit(solution)/shard_map/all_to_all | solution.py:72
